TPU v7x, 128 devices: a whole 4x4x4 slice. The times are simulated.
128 devices in a mesh: wide: 8 (over z, x_hi), narrow: 4 (over y), depth: 4 (over x_lo, core).
Axes of the slice: x: 4 (x_hi: 2, x_lo: 2; x = x_hi * 2 + x_lo), y: 4, z: 4, core: 2. Of those that a mesh axis runs over, the one named last changes fastest.
Arguments:
- hidden_in: bfloat16 [2048, 4096], P(('wide', 'narrow'), 'depth'), may hold values from -36 to 36
- queries: bfloat16 [2048, 4096], P('wide', ('narrow', 'depth')), may hold values from -8 to 8
- lang_ids: int32 [2048], replicated, may hold values from 0 to 7
- owner_slot: int32 [8], replicated, may hold values from 0 to 7, each once
- enc_kv: bfloat16 [8, 2, 768, 4096], P('wide', None, None, ('narrow', 'depth')), may hold values from -7 to 7
- attn_proj: bfloat16 [4096, 4096], P(('narrow', 'depth')), may hold values from -0.09375 to 0.09375
- norm_gain: float32 [4096], replicated, may hold values from 0.25 to 1.75
- router_proj: float32 [4096, 4], replicated, may hold values from -0.09375 to 0.09375
- expert_ids: int32 [2048, 2], P('wide'), may hold values from 0 to 3, all different within a row; in each aligned block of 64 rows (0 to 63, 64 to 127, ...) at most 48 rows name the same one
- proj_in: bfloat16 [4, 4096, 5120], P('narrow', None, 'depth'), may hold values from -0.09375 to 0.09375
- proj_out: bfloat16 [4, 5120, 4096], P('narrow', 'depth'), may hold values from -0.078125 to 0.078125
Outputs:
- layer_out: bfloat16 [2048, 4096], P(('wide', 'narrow'), 'depth')
Inputs may be any that keep to these rules, and one draw needn't show every extreme that they name: `owner_slot`: every slot once. `expert_ids`: each row names two different experts. Within each aligned block of 64 rows (the rows of one index of wide+narrow) no expert is named more than 48 times, a bound that some block reaches.
All inputs are finite; a program needn't handle non-finite values.
Results may differ from a plain program's by a relative error of at most 0.017.
Values may be sent and summed in bfloat16 or wider, within the bound.
No kernel may reach another device: no remote copies, remote signals or barrier semaphores. Data moves between devices by JAX's collectives and lax.ppermute only.
A program may use at most 128 MiB of HBM per device.

v0:
```python
import math
import jax
import jax.numpy as jnp
from jax import lax
from jax.sharding import PartitionSpec as P

HEAD_DIM = 64
CAP = 48
neg_big = -1e30
norm_eps = 1e-06


def in_order(blocks, dim):
    shape = list(blocks.shape[1:])
    shape[dim] *= blocks.shape[0]
    return jnp.moveaxis(blocks, 0, dim).reshape(shape)


def sent_to_all(value, axis):
    peers = lax.axis_size(axis)
    return lax.all_to_all(
        jnp.broadcast_to(value[None], (peers, *value.shape)), axis, 0, 0, tiled=True
    )


def collect(value, axis, dim):
    return in_order(sent_to_all(value, axis), dim)


def in_blocks(value, dim, peers):
    before, after = (value.shape[:dim], value.shape[dim + 1 :])
    return jnp.moveaxis(value.reshape(*before, peers, -1, *after), dim, 0)


def sum_at_owner(value, axis, dim):
    blocks = in_blocks(value, dim, lax.axis_size(axis))
    arrived = lax.all_to_all(blocks, axis, split_axis=0, concat_axis=0, tiled=True)
    return arrived.astype(jnp.float32).sum(axis=0)


def empty_state(row_count, head_count):
    return (
        jnp.full((row_count, head_count), neg_big, jnp.float32),
        jnp.zeros((row_count, head_count), jnp.float32),
        jnp.zeros((row_count, head_count, HEAD_DIM), jnp.float32),
    )


def slot_update(running, query_rows, key_rows, value_rows, is_live):
    run_max, run_sum, run_acc = running
    scores = jnp.einsum(
        "rhd,khd->rhk", query_rows, key_rows, preferred_element_type=jnp.float32
    ) * HEAD_DIM ** (-0.5)
    new_max = jnp.where(is_live[:, None], jnp.maximum(run_max, jnp.max(scores, axis=2)), run_max)
    weights = jnp.where(is_live[:, None, None], jnp.exp(scores - new_max[:, :, None]), 0.0)
    shrink = jnp.exp(run_max - new_max)
    run_sum = run_sum * shrink + jnp.sum(weights, axis=2)
    taken_sum = jnp.einsum(
        "rhk,khd->rhd", weights.astype(jnp.bfloat16), value_rows, preferred_element_type=jnp.float32
    )
    return (new_max, run_sum, run_acc * shrink[:, :, None] + taken_sum)


def slot_scan(running, kv_block, first_slot, query_rows, slot_tags):
    head_count = query_rows.shape[1]

    def visit_slot(carried, element):
        kv_pair, position = element
        key_rows = kv_pair[0].reshape(kv_pair.shape[1], head_count, HEAD_DIM)
        value_rows = kv_pair[1].reshape(kv_pair.shape[1], head_count, HEAD_DIM)
        return (slot_update(carried, query_rows, key_rows, value_rows, slot_tags == position), None)

    positions = first_slot + jnp.arange(kv_block.shape[0], dtype=jnp.int32)
    running, _ = lax.scan(visit_slot, running, (kv_block, positions))
    return running


def finish(running):
    run_max, run_sum, run_acc = running
    safe_sum = jnp.where(run_sum > 0.0, run_sum, 1.0)
    return (run_acc / safe_sum[:, :, None]).reshape(run_acc.shape[0], -1)


def assign_slots(choice_ids, experts):
    pick_flags = (
        choice_ids[:, :, None] == jnp.arange(experts, dtype=jnp.int32)[None, None, :]
    ).astype(jnp.int32)
    flat_flags = pick_flags.reshape(-1, experts)
    before = jnp.cumsum(flat_flags, axis=0) - flat_flags
    slot_rank = jnp.sum(before * flat_flags, axis=1).reshape(choice_ids.shape)
    return choice_ids * CAP + slot_rank


def make_worker(proj_in, proj_out, depth_count, quarter):
    experts_here = proj_in.shape[0]
    out_blocks = proj_out.reshape(experts_here, proj_out.shape[1], depth_count, quarter)

    def expert_ffn(arrived):
        sources = arrived.shape[0] // experts_here
        slot_count = arrived.shape[1]
        grid_rows = arrived.reshape(sources, experts_here, slot_count, arrived.shape[2])
        hidden_act = jnp.einsum(
            "secd,edf->secf", grid_rows, proj_in, preferred_element_type=jnp.float32
        )
        hidden_act = jax.nn.gelu(hidden_act, approximate=True).astype(jnp.bfloat16)
        expert_part = jnp.einsum(
            "secf,efgq->gsecq", hidden_act, out_blocks, preferred_element_type=jnp.float32
        )
        expert_part = expert_part.reshape(depth_count, sources * experts_here, slot_count, quarter)
        return expert_part

    return expert_ffn


def shards(
    hidden_in,
    queries,
    lang_ids,
    owner_slot,
    enc_kv,
    attn_proj,
    norm_gain,
    router_proj,
    expert_ids,
    proj_in,
    proj_out,
):
    narrow_count = lax.axis_size("narrow")
    depth_count = lax.axis_size("depth")
    tok_rows = hidden_in.shape[0]
    quarter = hidden_in.shape[1]
    head_count = queries.shape[1] // HEAD_DIM
    lang_count = owner_slot.shape[0]
    experts_here = proj_in.shape[0]
    experts = experts_here * narrow_count
    lang_match = lang_ids[:, None] == jnp.arange(lang_count, dtype=jnp.int32)[None, :]
    holder = jnp.sum(jnp.where(lang_match, owner_slot[None, :], 0), axis=1)
    first_slot = lax.axis_index("wide") * enc_kv.shape[0]
    segment = collect(queries, "wide", 0)
    row_count = segment.shape[0]
    block_rows = math.gcd(row_count, 512)

    def one_block(element):
        part_rows, part_tags = element
        running = slot_scan(
            empty_state(block_rows, head_count),
            enc_kv,
            first_slot,
            part_rows.reshape(block_rows, head_count, HEAD_DIM),
            part_tags,
        )
        return finish(running)

    blocks_out = lax.map(
        one_block,
        (
            segment.reshape(row_count // block_rows, block_rows, segment.shape[1]),
            holder.reshape(row_count // block_rows, block_rows),
        ),
    )
    partial_context = blocks_out.reshape(row_count, segment.shape[1])
    context = sum_at_owner(partial_context.astype(jnp.bfloat16), "wide", 0).astype(jnp.bfloat16)
    context_blocks = context.reshape(narrow_count, tok_rows, context.shape[1])
    proj_blocks = attn_proj.reshape(attn_proj.shape[0], depth_count, quarter)

    def pair_term(pair_index):
        row_block = lax.dynamic_index_in_dim(
            context_blocks, pair_index // depth_count, 0, keepdims=False
        )
        col_block = lax.dynamic_index_in_dim(
            proj_blocks, pair_index % depth_count, 1, keepdims=False
        )
        return jnp.dot(row_block, col_block, preferred_element_type=jnp.float32)

    pair_ids = jnp.arange(
        tok_rows * lax.axis_size(("narrow", "depth")) // tok_rows, dtype=jnp.int32
    )
    attn_out = sum_at_owner(
        lax.map(pair_term, pair_ids)
        .reshape(tok_rows * lax.axis_size(("narrow", "depth")), quarter)
        .astype(jnp.bfloat16),
        ("narrow", "depth"),
        0,
    )
    residual = (hidden_in.astype(jnp.float32) + attn_out).astype(jnp.bfloat16)
    full_rows = lax.all_gather(residual, "depth", axis=1, tiled=True).astype(jnp.float32)
    inv_norm = lax.rsqrt(jnp.mean(full_rows * full_rows, axis=1) + norm_eps)
    normed = (full_rows * inv_norm[:, None] * norm_gain[None, :]).astype(jnp.bfloat16)
    narrow_at = lax.axis_index("narrow")
    own_ids = lax.dynamic_slice_in_dim(expert_ids, narrow_at * tok_rows, tok_rows, 0)
    targets = assign_slots(own_ids, experts)
    lane_ids = jnp.arange(experts * CAP, dtype=jnp.int32)
    dispatch_mask = jnp.any(lane_ids[:, None, None] == targets[None, :, :], axis=2).astype(
        jnp.bfloat16
    )
    outbox = jnp.dot(dispatch_mask, normed, preferred_element_type=jnp.float32).astype(jnp.bfloat16)
    outbox = outbox.reshape(experts, CAP, normed.shape[1])
    worker = make_worker(proj_in, proj_out, depth_count, quarter)
    arrived_out = worker(lax.all_to_all(outbox, "narrow", split_axis=0, concat_axis=0, tiled=True))
    summed = sum_at_owner(arrived_out.astype(jnp.bfloat16), "depth", 0)
    returned = lax.all_to_all(
        summed.astype(jnp.bfloat16), "narrow", split_axis=1, concat_axis=1, tiled=True
    ).astype(summed.dtype)
    logits = jnp.dot(normed.astype(jnp.float32), router_proj, precision=lax.Precision.HIGHEST)
    pick_mask = own_ids[:, :, None] == jnp.arange(experts, dtype=jnp.int32)[None, None, :]
    own_logit = jnp.sum(jnp.where(pick_mask, logits[:, None, :], 0.0), axis=2)
    gates = jax.nn.sigmoid(own_logit - own_logit[:, ::-1])
    picked = jnp.take(
        returned.reshape(experts * CAP, quarter), targets.reshape(-1), axis=0
    ).reshape(tok_rows, 2, quarter)
    combined = jnp.sum(gates[:, :, None] * picked, axis=1)
    return (residual.astype(jnp.float32) + combined).astype(jnp.bfloat16)


def solution(mesh):
    return jax.shard_map(
        shards,
        mesh=mesh,
        in_specs=(
            P(("wide", "narrow"), "depth"),
            P("wide", ("narrow", "depth")),
            P(),
            P(),
            P("wide", None, None, ("narrow", "depth")),
            P(("narrow", "depth"), None),
            P(),
            P(),
            P("wide", None),
            P("narrow", None, "depth"),
            P("narrow", "depth", None),
        ),
        out_specs=P(("wide", "narrow"), "depth"),
        check_vma=False,
    )
```

profile of v0, /device:TPU:0, one launch (start us, length us, event | category | flops | bytes accessed | tf_op | source)
XLA Modules:
  0.0 258.0 jit_solution(7034597366299841906)
XLA Ops:
  0.0 2.0 broadcast_in_dim.114
  2.0 7.9 %all-to-all-start = ((bf16[8,256,256]{2,1,0:T(8,128)(2,1)}), bf16[8,256,256]{2,1,0:T(8,128)(2,1)S(1)}, u32[]{:S(2)}, u32[]{:S(2)}) async-start(bf16[8,256,256]{2,1,0:T(8,128)(2,1)} %broadcast_in_dim.114), calls=%async_computation | async-start | bytes 2097152 | tf_op jit(solution)/shard_map/all_to_all | solution.py:21
  10.7 1.4 copy.51
  12.1 15.0 %all-to-all-done = bf16[8,256,256]{2,1,0:T(8,128)(2,1)S(1)} async-done(((bf16[8,256,256]{2,1,0:T(8,128)(2,1)}), bf16[8,256,256]{2,1,0:T(8,128)(2,1)S(1)}, u32[]{:S(2)}, u32[]{:S(2)}) %all-to-all-start) | async-done | bytes 1048608 | tf_op jit(solution)/shard_map/all_to_all | solution.py:21
  27.1 20.3 %while.28 = (s32[]{:T(128)}, bf16[4,512,256]{2,1,0:T(8,128)(2,1)S(1)}, s32[4,512]{1,0:T(4,128)S(1)}, s32[]{:T(128)}, bf16[4,512,256]{2,1,0:T(8,128)(2,1)S(1)}, /*index=5*/bf16[1,2,768,256]{2,3,1,0:T(8,128)(2,1)S(1)}, s32[]{:T(128)}) while((s32[]{:T(128)}, bf16[4,512,256]{2,1,0:T(8,128)(2,1)S(1)}, s32[4,512]{1,0:T(4,128)S(1)}, s32[]{:T(128)}, ...), condition=%wide.region_4.5_spmd, body=%wide.region_1.4_spmd.sunk | while | flops 418789888 | bytes 23957604 | solution.py:154
  27.3 1.1 bitcast_reduce_fusion.2
  28.5 1.7 fusion.94
  30.2 1.8 fusion.95
  32.4 1.1 bitcast_reduce_fusion.2
  33.6 1.7 fusion.94
  35.3 1.8 fusion.95
  37.5 1.1 bitcast_reduce_fusion.2
  38.6 1.7 fusion.94
  40.3 1.8 fusion.95
  42.6 1.1 bitcast_reduce_fusion.2
  43.7 1.7 fusion.94
  45.4 1.8 fusion.95
  47.4 1.0 copy-done.1
  48.4 3.6 %all-to-all-start.1 = ((bf16[8,256,256]{2,1,0:T(8,128)(2,1)}), bf16[8,256,256]{2,1,0:T(8,128)(2,1)S(1)}, u32[]{:S(2)}, u32[]{:S(2)}) async-start(bf16[8,256,256]{2,1,0:T(8,128)(2,1)} %bitcast.143), calls=%async_computation.1 | async-start | bytes 2097152 | tf_op jit(solution)/shard_map/all_to_all | solution.py:37
  51.9 3.3 %copy.53 = bf16[256,4096]{0,1:T(8,128)(2,1)S(1)} copy(bf16[256,4096]{1,0:T(8,128)(2,1)} %param.20) | data formatting | bytes 4194304 | tf_op args[5]
  55.2 13.2 %all-to-all-done.1 = bf16[8,256,256]{2,1,0:T(8,128)(2,1)S(1)} async-done(((bf16[8,256,256]{2,1,0:T(8,128)(2,1)}), bf16[8,256,256]{2,1,0:T(8,128)(2,1)S(1)}, u32[]{:S(2)}, u32[]{:S(2)}) %all-to-all-start.1) | async-done | bytes 1048608 | tf_op jit(solution)/shard_map/all_to_all | solution.py:37
  68.6 64.6 %while.29 = (s32[]{:T(128)}, bf16[16,64,1024]{2,1,0:T(8,128)(2,1)}, s32[16]{0:T(128)S(1)}, bf16[4,64,256]{2,1,0:T(8,128)(2,1)S(1)}, bf16[256,4,1024]{0,2,1:T(8,1...) while((s32[]{:T(128)}, bf16[16,64,1024]{2,1,0:T(8,128)(2,1)}, ...), condition=%wide.region_7.8_spmd, body=%wide.region_6.7_spmd.sunk | while | flops 33554456 | bytes 819596 | solution.py:179
  75.8 0.9 fusion.98
  79.8 1.0 fusion.98
  83.9 0.9 fusion.98
  87.9 0.9 fusion.98
  96.0 0.9 fusion.98
  100.0 1.0 fusion.98
  104.1 0.9 fusion.98
  108.1 0.9 fusion.98
  112.1 0.9 fusion.98
  116.2 0.9 fusion.98
  124.2 0.9 fusion.98
  132.3 0.9 fusion.98
  133.3 4.6 %all-to-all-start.2 = ((bf16[16,64,1024]{2,1,0:T(8,128)(2,1)}), bf16[16,64,1024]{2,1,0:T(8,128)(2,1)S(1)}, u32[]{:S(2)}, u32[]{:S(2)}) async-start(bf16[16,64,1024]{2,1,0:T(8,128)(2,1)} %get-tuple-element.130), calls=%async_computation.2 | async-start | bytes 4194304 | tf_op jit(solution)/shard_map/all_to_all | solution.py:37
  139.1 26.6 %all-to-all-done.2 = bf16[16,64,1024]{2,1,0:T(8,128)(2,1)S(1)} async-done(((bf16[16,64,1024]{2,1,0:T(8,128)(2,1)}), bf16[16,64,1024]{2,1,0:T(8,128)(2,1)S(1)}, u32[]{:S(2)}, u32[]{:S(2)}) %all-to-all-start.2) | async-done | bytes 2097184 | tf_op jit(solution)/shard_map/all_to_all | solution.py:37
  166.1 6.5 %all_gather.3 = bf16[64,4096]{1,0:T(8,128)(2,1)S(1)} all-gather(bf16[64,1024]{1,0:T(8,128)(2,1)S(1)} %add_convert_fusion.1), channel_id=1, replica_groups=mesh['wide'=8,'narrow'=4,'depth'=4] {'depth'}, dimensions={1}, use_global_device_ids=true | all-gather | bytes 655360 | tf_op jit(solution)/shard_map/all_gather | solution.py:186
  172.8 1.8 convolution_convert_fusion
  174.6 3.7 %all-to-all-start.3 = ((bf16[4,48,4096]{2,1,0:T(8,128)(2,1)}), bf16[4,48,4096]{2,1,0:T(8,128)(2,1)S(1)}, u32[]{:S(2)}, u32[]{:S(2)}) async-start(bf16[4,48,4096]{2,1,0:T(8,128)(2,1)} %bitcast.14), calls=%async_computation.3 | async-start | bytes 3145728 | tf_op jit(solution)/shard_map/all_to_all | solution.py:199
  178.4 17.8 %reshape.205 = bf16[1280,4,1024]{2,1,0:T(4,128)(2,1)} reshape(bf16[1,1280,4096]{2,1,0:T(8,128)(2,1)} %param.25) | data formatting | bytes 20971520 | tf_op jit(solution)/shard_map/reshape.14
  196.2 3.5 %all-to-all-done.3 = bf16[4,48,4096]{2,1,0:T(8,128)(2,1)S(1)} async-done(((bf16[4,48,4096]{2,1,0:T(8,128)(2,1)}), bf16[4,48,4096]{2,1,0:T(8,128)(2,1)S(1)}, u32[]{:S(2)}, u32[]{:S(2)}) %all-to-all-start.3) | async-done | bytes 1572896 | tf_op jit(solution)/shard_map/all_to_all | solution.py:199
  199.7 16.7 %fusion.35 = bf16[4,1,4,48,1024]{4,3,0,2,1:T(8,128)(2,1)} fusion(bf16[1280,4,1024]{2,1,0:T(4,128)(2,1)} %reshape.205, bf16[4,48,4096]{2,1,0:T(8,128)(2,1)S(1)} %all-to-all-done.3, bf16[1,4096,1280]{2,1,0:T(8,128)(2,1)} %param.24), kind=kOutput, calls=%fused_computation.36 | convolution fusion | flops 4029530112 | bytes 24117248 | tf_op jit(solution)/shard_map/secf,efgq->gsecq/dot_general | solution.py:106
  216.4 2.7 %copy.60 = bf16[4,1,4,48,1024]{4,3,2,1,0:T(8,128)(2,1)} copy(bf16[4,1,4,48,1024]{4,3,0,2,1:T(8,128)(2,1)} %fusion.35) | data formatting | bytes 3145728 | tf_op jit(solution)/shard_map/convert_element_type | solution.py:200
  219.1 3.6 %all-to-all-start.4 = ((bf16[4,1,4,48,1024]{4,3,2,1,0:T(8,128)(2,1)}), bf16[4,1,4,48,1024]{4,3,2,1,0:T(8,128)(2,1)S(1)}, u32[]{:S(2)}, u32[]{:S(2)}) async-start(bf16[4,1,4,48,1024]{4,3,2,1,0:T(8,128)(2,1)} %copy.60), calls=%async_computation.4 | async-start | bytes 3145728 | tf_op jit(solution)/shard_map/all_to_all | solution.py:37
  223.6 19.0 %all-to-all-done.4 = bf16[4,1,4,48,1024]{4,3,2,1,0:T(8,128)(2,1)S(1)} async-done(((bf16[4,1,4,48,1024]{4,3,2,1,0:T(8,128)(2,1)}), bf16[4,1,4,48,1024]{4,3,2,1,0:T(8,128)(2,1)S(1)}, u32[]{:S(2)}, u32[]{:S(2)}) %all-to-all-start.4) | async-done | bytes 1572896 | tf_op jit(solution)/shard_map/all_to_all | solution.py:37
  242.7 1.1 reduce_sum.96
  243.8 3.5 %all-to-all-start.5 = ((bf16[1,4,48,1024]{3,2,0,1:T(8,128)(2,1)}), bf16[1,4,48,1024]{3,2,0,1:T(8,128)(2,1)S(1)}, u32[]{:S(2)}, u32[]{:S(2)}) async-start(bf16[1,4,48,1024]{3,2,0,1:T(8,128)(2,1)} %bitcast.30), calls=%async_computation.5 | async-start | bytes 786432 | tf_op jit(solution)/shard_map/all_to_all | solution.py:201
  247.4 7.9 %all-to-all-done.5 = bf16[1,4,48,1024]{3,2,0,1:T(8,128)(2,1)S(1)} async-done(((bf16[1,4,48,1024]{3,2,0,1:T(8,128)(2,1)}), bf16[1,4,48,1024]{3,2,0,1:T(8,128)(2,1)S(1)}, u32[]{:S(2)}, u32[]{:S(2)}) %all-to-all-start.5) | async-done | bytes 393248 | tf_op jit(solution)/shard_map/all_to_all | solution.py:201
  (96 shorter events, 21.5 us)
Async XLA Ops:
  0.0 223.0 %copy-start = (f32[4096,4]{0,1:T(4,128)S(1)}, f32[4096,4]{0,1:T(4,128)}, u32[]{:S(2)}) copy-start(f32[4096,4]{0,1:T(4,128)} %param.22) | copy-start | bytes 196612
  2.0 25.1 %all-to-all-start = ((bf16[8,256,256]{2,1,0:T(8,128)(2,1)}), bf16[8,256,256]{2,1,0:T(8,128)(2,1)S(1)}, u32[]{:S(2)}, u32[]{:S(2)}) async-start(bf16[8,256,256]{2,1,0:T(8,128)(2,1)} %broadcast_in_dim.114), calls=%async_computation | async-start | bytes 2097152 | tf_op jit(solution)/shard_map/all_to_all | solution.py:21
  47.4 1.0 copy-start.1
  48.4 20.1 %all-to-all-start.1 = ((bf16[8,256,256]{2,1,0:T(8,128)(2,1)}), bf16[8,256,256]{2,1,0:T(8,128)(2,1)S(1)}, u32[]{:S(2)}, u32[]{:S(2)}) async-start(bf16[8,256,256]{2,1,0:T(8,128)(2,1)} %bitcast.143), calls=%async_computation.1 | async-start | bytes 2097152 | tf_op jit(solution)/shard_map/all_to_all | solution.py:37
  51.9 85.9 %copy-start.4 = (s32[256,2]{0,1:T(2,128)S(1)}, s32[256,2]{0,1:T(2,128)}, u32[]{:S(2)}) copy-start(s32[256,2]{0,1:T(2,128)} %param.23) | copy-start | bytes 6148
  55.2 110.8 %copy-start.2 = (bf16[64,1024]{1,0:T(8,128)(2,1)S(1)}, bf16[64,1024]{1,0:T(8,128)(2,1)}, u32[]{:S(2)}) copy-start(bf16[64,1024]{1,0:T(8,128)(2,1)} %param.15) | copy-start | bytes 393220
  68.6 104.2 %copy-start.3 = (f32[4096]{0:T(1024)S(1)}, f32[4096]{0:T(1024)}, u32[]{:S(2)}) copy-start(f32[4096]{0:T(1024)} %param.21) | copy-start | bytes 49156
  133.3 32.4 %all-to-all-start.2 = ((bf16[16,64,1024]{2,1,0:T(8,128)(2,1)}), bf16[16,64,1024]{2,1,0:T(8,128)(2,1)S(1)}, u32[]{:S(2)}, u32[]{:S(2)}) async-start(bf16[16,64,1024]{2,1,0:T(8,128)(2,1)} %get-tuple-element.130), calls=%async_computation.2 | async-start | bytes 4194304 | tf_op jit(solution)/shard_map/all_to_all | solution.py:37
  174.6 25.0 %all-to-all-start.3 = ((bf16[4,48,4096]{2,1,0:T(8,128)(2,1)}), bf16[4,48,4096]{2,1,0:T(8,128)(2,1)S(1)}, u32[]{:S(2)}, u32[]{:S(2)}) async-start(bf16[4,48,4096]{2,1,0:T(8,128)(2,1)} %bitcast.14), calls=%async_computation.3 | async-start | bytes 3145728 | tf_op jit(solution)/shard_map/all_to_all | solution.py:199
  219.1 23.6 %all-to-all-start.4 = ((bf16[4,1,4,48,1024]{4,3,2,1,0:T(8,128)(2,1)}), bf16[4,1,4,48,1024]{4,3,2,1,0:T(8,128)(2,1)S(1)}, u32[]{:S(2)}, u32[]{:S(2)}) async-start(bf16[4,1,4,48,1024]{4,3,2,1,0:T(8,128)(2,1)} %copy.60), calls=%async_computation.4 | async-start | bytes 3145728 | tf_op jit(solution)/shard_map/all_to_all | solution.py:37
  243.8 11.5 %all-to-all-start.5 = ((bf16[1,4,48,1024]{3,2,0,1:T(8,128)(2,1)}), bf16[1,4,48,1024]{3,2,0,1:T(8,128)(2,1)S(1)}, u32[]{:S(2)}, u32[]{:S(2)}) async-start(bf16[1,4,48,1024]{3,2,0,1:T(8,128)(2,1)} %bitcast.30), calls=%async_computation.5 | async-start | bytes 786432 | tf_op jit(solution)/shard_map/all_to_all | solution.py:201
where the time goes:
time: 260 us; the launch traced here: 258 us
  waiting for transfers between devices  85.2 us (33%)
  matrix products  45.8 us (18%)
  local copies, waits for them, and re-layouts  41.3 us (16%)
  loops' own time  40.3 us (15%)
  starting transfers between devices  26.8 us (10%)
  other arithmetic  11.9 us (5%)
  blocking collectives  6.5 us (2%)
    all_to_all x3, waiting for transfers between devices, sum_at_owner(): lax.all_to_all(blocks, axis, split_axis=0, concat_axis=0, tiled=True)  58.9 us
    another operation x1, loops' own time, shards(): lax.map(pair_term, pair_ids)  40.1 us
    another operation x1, local copies, waits for them, and re-layouts  17.8 us
    dot_general x1, matrix products, expert_ffn(): jnp.einsum('secf,efgq->gsecq', hidden_act, out_blocks, preferred_element_...  16.7 us
    dot_general x16, matrix products, pair_term(): return jnp.dot(row_block, col_block, preferred_element_type=jnp.float32)  15.1 us
    all_to_all x1, waiting for transfers between devices, sent_to_all(): lax.all_to_all(jnp.broadcast_to(value[None], (peers, *value.shape)), axis...  15 us
    all_to_all x3, starting transfers between devices, sum_at_owner(): lax.all_to_all(blocks, axis, split_axis=0, concat_axis=0, tiled=True)  11.7 us
    dynamic_slice x16, local copies, waits for them, and re-layouts, shards(): lax.map(pair_term, pair_ids)  9.44 us
  transfers between devices with their start and end apart: 6, of which 6 were waited for; matrix products, arithmetic and copies ran while one was open for 10% of the time, Pallas kernels for 0%

commit v1 on v0

--- a/solution.py
+++ b/solution.py
@@ -183,7 +183,9 @@
         0,
     )
     residual = (hidden_in.astype(jnp.float32) + attn_out).astype(jnp.bfloat16)
-    full_rows = lax.all_gather(residual, "depth", axis=1, tiled=True).astype(jnp.float32)
+    full_rows = jnp.concatenate(
+        lax.all_to_all(jnp.stack(lax.axis_size("depth") * [residual], 0), "depth", 0, 0), 1
+    ).astype(jnp.float32)
     inv_norm = lax.rsqrt(jnp.mean(full_rows * full_rows, axis=1) + norm_eps)
     normed = (full_rows * inv_norm[:, None] * norm_gain[None, :]).astype(jnp.bfloat16)
     narrow_at = lax.axis_index("narrow")

time: 260 us -> 271 us (1.042)
  waiting for transfers between devices: 85.2 us -> 93.4 us
  blocking collectives: 6.5 us -> 0 us
  starting transfers between devices: 26.8 us -> 32 us
  local copies, waits for them, and re-layouts: 41.3 us -> 44.1 us
    all_to_all x0 -> x1, waiting for transfers between devices: none -> 8.19 us  [shards(): lax.all_to_all(jnp.stack(lax.axis_size('depth') * [residual], 0), 'depth'...]
    all_gather x1 -> x0, blocking collectives: 6.5 us -> none  [shards(): lax.all_gather(residual, 'depth', axis=1, tiled=True).astype(jnp.float32)]
    all_to_all x0 -> x1, starting transfers between devices: none -> 3.47 us  [shards(): lax.all_to_all(jnp.stack(lax.axis_size('depth') * [residual], 0), 'depth'...]
    dynamic_update_slice x8, local copies, waits for them, and re-layouts: 0.63 us -> 3.47 us  [shards(): lax.map(one_block, (segment.reshape(row_count // block_rows, block_rows,...]
    another operation x1 -> x2, local copies, waits for them, and re-layouts: 17.8 us -> 18.7 us
  transfers between devices with their start and end apart: 6 -> 7, of which waited for: 6 -> 7; matrix products, arithmetic and copies ran while one was open for 10% -> 9% of each run, Pallas kernels for 0% -> 0%
where the time goes in v1:
time: 271 us; the launch traced here: 270 us
  waiting for transfers between devices  93.4 us (34%)
  matrix products  46.3 us (17%)
  local copies, waits for them, and re-layouts  44.1 us (16%)
  loops' own time  40.3 us (15%)
  starting transfers between devices  32 us (12%)
  other arithmetic  13.4 us (5%)
    all_to_all x3, waiting for transfers between devices, sum_at_owner(): lax.all_to_all(blocks, axis, split_axis=0, concat_axis=0, tiled=True)  59.6 us
    another operation x1, loops' own time, shards(): lax.map(pair_term, pair_ids)  40 us
    another operation x1, local copies, waits for them, and re-layouts  17.8 us
    dot_general x1, matrix products, expert_ffn(): jnp.einsum('secf,efgq->gsecq', hidden_act, out_blocks, preferred_element_...  17.2 us
    dot_general x16, matrix products, pair_term(): return jnp.dot(row_block, col_block, preferred_element_type=jnp.float32)  15.1 us
    all_to_all x1, waiting for transfers between devices, sent_to_all(): lax.all_to_all(jnp.broadcast_to(value[None], (peers, *value.shape)), axis...  15 us
    all_to_all x3, starting transfers between devices, sum_at_owner(): lax.all_to_all(blocks, axis, split_axis=0, concat_axis=0, tiled=True)  12.6 us
    dynamic_slice x16, local copies, waits for them, and re-layouts, shards(): lax.map(pair_term, pair_ids)  9.44 us
  transfers between devices with their start and end apart: 7, of which 7 were waited for; matrix products, arithmetic and copies ran while one was open for 9% of the time, Pallas kernels for 0%

profile of v1, /device:TPU:0, one launch (start us, length us, event | category | flops | bytes accessed | tf_op | source)
XLA Modules:
  0.0 269.7 jit_solution(4706272069725545494)
XLA Ops:
  0.0 2.0 broadcast_in_dim.114
  2.0 7.9 %all-to-all-start = ((bf16[8,256,256]{2,1,0:T(8,128)(2,1)}), bf16[8,256,256]{2,1,0:T(8,128)(2,1)S(1)}, u32[]{:S(2)}, u32[]{:S(2)}) async-start(bf16[8,256,256]{2,1,0:T(8,128)(2,1)} %broadcast_in_dim.114), calls=%async_computation | async-start | bytes 2097152 | tf_op jit(solution)/shard_map/all_to_all | solution.py:21
  10.7 1.4 copy.53
  12.1 15.0 %all-to-all-done = bf16[8,256,256]{2,1,0:T(8,128)(2,1)S(1)} async-done(((bf16[8,256,256]{2,1,0:T(8,128)(2,1)}), bf16[8,256,256]{2,1,0:T(8,128)(2,1)S(1)}, u32[]{:S(2)}, u32[]{:S(2)}) %all-to-all-start) | async-done | bytes 1048608 | tf_op jit(solution)/shard_map/all_to_all | solution.py:21
  27.1 23.0 %while.28 = (s32[]{:T(128)}, bf16[4,512,256]{2,1,0:T(8,128)(2,1)}, s32[4,512]{1,0:T(4,128)S(1)}, s32[]{:T(128)}, bf16[4,512,256]{2,1,0:T(8,128)(2,1)S(1)}, /*index=5*/bf16[1,2,768,256]{2,3,1,0:T(8,128)(2,1)S(1)}, s32[]{:T(128)}) while((s32[]{:T(128)}, bf16[4,512,256]{2,1,0:T(8,128)(2,1)}, s32[4,512]{1,0:T(4,128)S(1)}, s32[]{:T(128)}, ...), condition=%wide.region_4.5_spmd, body=%wide.region_1.4_spmd.sunk | while | flops 418789888 | bytes 23957604 | solution.py:154
  27.3 1.1 bitcast_reduce_fusion.2
  28.5 1.7 fusion.90
  30.2 1.8 fusion.91
  33.1 1.1 bitcast_reduce_fusion.2
  34.2 1.7 fusion.90
  35.9 1.8 fusion.91
  38.8 1.1 bitcast_reduce_fusion.2
  40.0 1.7 fusion.90
  41.7 1.8 fusion.91
  44.6 1.1 bitcast_reduce_fusion.2
  45.7 1.7 fusion.90
  47.4 1.8 fusion.91
  50.1 3.6 %all-to-all-start.1 = ((bf16[8,256,256]{2,1,0:T(8,128)(2,1)}), bf16[8,256,256]{2,1,0:T(8,128)(2,1)S(1)}, u32[]{:S(2)}, u32[]{:S(2)}) async-start(bf16[8,256,256]{2,1,0:T(8,128)(2,1)} %bitcast.150), calls=%async_computation.1 | async-start | bytes 2097152 | tf_op jit(solution)/shard_map/all_to_all | solution.py:37
  53.7 3.3 %copy.55 = bf16[256,4096]{0,1:T(8,128)(2,1)S(1)} copy(bf16[256,4096]{1,0:T(8,128)(2,1)} %param.20) | data formatting | bytes 4194304 | tf_op args[5]
  56.9 13.2 %all-to-all-done.1 = bf16[8,256,256]{2,1,0:T(8,128)(2,1)S(1)} async-done(((bf16[8,256,256]{2,1,0:T(8,128)(2,1)}), bf16[8,256,256]{2,1,0:T(8,128)(2,1)S(1)}, u32[]{:S(2)}, u32[]{:S(2)}) %all-to-all-start.1) | async-done | bytes 1048608 | tf_op jit(solution)/shard_map/all_to_all | solution.py:37
  70.3 64.6 %while.29 = (s32[]{:T(128)}, bf16[16,64,1024]{2,1,0:T(8,128)(2,1)}, s32[16]{0:T(128)S(1)}, bf16[4,64,256]{2,1,0:T(8,128)(2,1)S(1)}, bf16[256,4,1024]{0,2,1:T(8,1...) while((s32[]{:T(128)}, bf16[16,64,1024]{2,1,0:T(8,128)(2,1)}, ...), condition=%wide.region_7.8_spmd, body=%wide.region_6.7_spmd.sunk | while | flops 33554456 | bytes 819596 | solution.py:179
  77.5 0.9 fusion.94
  81.5 1.0 fusion.94
  85.6 0.9 fusion.94
  89.6 0.9 fusion.94
  97.7 0.9 fusion.94
  101.7 1.0 fusion.94
  105.8 0.9 fusion.94
  109.8 0.9 fusion.94
  113.8 0.9 fusion.94
  117.9 0.9 fusion.94
  125.9 0.9 fusion.94
  134.0 0.9 fusion.94
  135.0 4.7 %all-to-all-start.2 = ((bf16[16,64,1024]{2,1,0:T(8,128)(2,1)}), bf16[16,64,1024]{2,1,0:T(8,128)(2,1)S(1)}, u32[]{:S(2)}, u32[]{:S(2)}) async-start(bf16[16,64,1024]{2,1,0:T(8,128)(2,1)} %get-tuple-element.130), calls=%async_computation.2 | async-start | bytes 4194304 | tf_op jit(solution)/shard_map/all_to_all | solution.py:37
  140.3 27.2 %all-to-all-done.2 = bf16[16,64,1024]{2,1,0:T(8,128)(2,1)S(1)} async-done(((bf16[16,64,1024]{2,1,0:T(8,128)(2,1)}), bf16[16,64,1024]{2,1,0:T(8,128)(2,1)S(1)}, u32[]{:S(2)}, u32[]{:S(2)}) %all-to-all-start.2) | async-done | bytes 2097184 | tf_op jit(solution)/shard_map/all_to_all | solution.py:37
  168.8 3.5 %all-to-all-start.3 = ((bf16[4,64,1024]{2,1,0:T(8,128)(2,1)}), bf16[4,64,1024]{2,1,0:T(8,128)(2,1)S(1)}, u32[]{:S(2)}, u32[]{:S(2)}) async-start(bf16[4,64,1024]{2,1,0:T(8,128)(2,1)} %stack.2), calls=%async_computation.3 | async-start | bytes 1048576 | tf_op jit(solution)/shard_map/all_to_all | solution.py:187
  172.9 8.2 %all-to-all-done.3 = bf16[4,64,1024]{2,1,0:T(8,128)(2,1)S(1)} async-done(((bf16[4,64,1024]{2,1,0:T(8,128)(2,1)}), bf16[4,64,1024]{2,1,0:T(8,128)(2,1)S(1)}, u32[]{:S(2)}, u32[]{:S(2)}) %all-to-all-start.3) | async-done | bytes 524320 | tf_op jit(solution)/shard_map/all_to_all | solution.py:187
  181.5 1.9 convolution_convert_fusion
  183.4 4.5 %all-to-all-start.4 = ((bf16[4,48,4096]{2,1,0:T(8,128)(2,1)}), bf16[4,48,4096]{2,1,0:T(8,128)(2,1)}, u32[]{:S(2)}, u32[]{:S(2)}) async-start(bf16[4,48,4096]{2,1,0:T(8,128)(2,1)} %bitcast.148), calls=%async_computation.4 | async-start | bytes 3145728 | tf_op jit(solution)/shard_map/all_to_all | solution.py:201
  187.9 17.8 %reshape.211 = bf16[1280,4,1024]{2,1,0:T(4,128)(2,1)} reshape(bf16[1,1280,4096]{2,1,0:T(8,128)(2,1)} %param.25) | data formatting | bytes 20971520 | tf_op jit(solution)/shard_map/reshape.15
  205.8 2.8 %all-to-all-done.4 = bf16[4,48,4096]{2,1,0:T(8,128)(2,1)} async-done(((bf16[4,48,4096]{2,1,0:T(8,128)(2,1)}), bf16[4,48,4096]{2,1,0:T(8,128)(2,1)}, u32[]{:S(2)}, u32[]{:S(2)}) %all-to-all-start.4) | async-done | bytes 1572896 | tf_op jit(solution)/shard_map/all_to_all | solution.py:201
  208.5 17.2 %fusion.35 = bf16[4,1,4,48,1024]{4,3,0,2,1:T(8,128)(2,1)} fusion(bf16[1280,4,1024]{2,1,0:T(4,128)(2,1)} %reshape.211, bf16[4,48,4096]{2,1,0:T(8,128)(2,1)} %all-to-all-done.4, bf16[1,4096,1280]{2,1,0:T(8,128)(2,1)} %param.24), kind=kOutput, calls=%fused_computation.36 | convolution fusion | flops 4029530112 | bytes 24117248 | tf_op jit(solution)/shard_map/secf,efgq->gsecq/dot_general | solution.py:106
  225.8 2.7 %copy.63 = bf16[4,1,4,48,1024]{4,3,2,1,0:T(8,128)(2,1)} copy(bf16[4,1,4,48,1024]{4,3,0,2,1:T(8,128)(2,1)} %fusion.35) | data formatting | bytes 3145728 | tf_op jit(solution)/shard_map/convert_element_type | solution.py:202
  228.5 4.3 %all-to-all-start.5 = ((bf16[4,1,4,48,1024]{4,3,2,1,0:T(8,128)(2,1)}), bf16[4,1,4,48,1024]{4,3,2,1,0:T(8,128)(2,1)}, u32[]{:S(2)}, u32[]{:S(2)}) async-start(bf16[4,1,4,48,1024]{4,3,2,1,0:T(8,128)(2,1)} %copy.63), calls=%async_computation.5 | async-start | bytes 3145728 | tf_op jit(solution)/shard_map/all_to_all | solution.py:37
  233.8 19.2 %all-to-all-done.5 = bf16[4,1,4,48,1024]{4,3,2,1,0:T(8,128)(2,1)} async-done(((bf16[4,1,4,48,1024]{4,3,2,1,0:T(8,128)(2,1)}), bf16[4,1,4,48,1024]{4,3,2,1,0:T(8,128)(2,1)}, u32[]{:S(2)}, u32[]{:S(2)}) %all-to-all-start.5) | async-done | bytes 1572896 | tf_op jit(solution)/shard_map/all_to_all | solution.py:37
  252.9 2.6 reduce_sum.96
  255.5 3.5 %all-to-all-start.6 = ((bf16[1,4,48,1024]{3,2,0,1:T(8,128)(2,1)}), bf16[1,4,48,1024]{3,2,0,1:T(8,128)(2,1)S(1)}, u32[]{:S(2)}, u32[]{:S(2)}) async-start(bf16[1,4,48,1024]{3,2,0,1:T(8,128)(2,1)} %bitcast.31), calls=%async_computation.6 | async-start | bytes 786432 | tf_op jit(solution)/shard_map/all_to_all | solution.py:203
  259.1 7.9 %all-to-all-done.6 = bf16[1,4,48,1024]{3,2,0,1:T(8,128)(2,1)S(1)} async-done(((bf16[1,4,48,1024]{3,2,0,1:T(8,128)(2,1)}), bf16[1,4,48,1024]{3,2,0,1:T(8,128)(2,1)S(1)}, u32[]{:S(2)}, u32[]{:S(2)}) %all-to-all-start.6) | async-done | bytes 393248 | tf_op jit(solution)/shard_map/all_to_all | solution.py:203
  (98 shorter events, 25.3 us)
Async XLA Ops:
  0.0 233.2 %copy-start = (f32[4096,4]{0,1:T(4,128)S(1)}, f32[4096,4]{0,1:T(4,128)}, u32[]{:S(2)}) copy-start(f32[4096,4]{0,1:T(4,128)} %param.22) | copy-start | bytes 196612
  2.0 25.1 %all-to-all-start = ((bf16[8,256,256]{2,1,0:T(8,128)(2,1)}), bf16[8,256,256]{2,1,0:T(8,128)(2,1)S(1)}, u32[]{:S(2)}, u32[]{:S(2)}) async-start(bf16[8,256,256]{2,1,0:T(8,128)(2,1)} %broadcast_in_dim.114), calls=%async_computation | async-start | bytes 2097152 | tf_op jit(solution)/shard_map/all_to_all | solution.py:21
  50.1 20.1 %all-to-all-start.1 = ((bf16[8,256,256]{2,1,0:T(8,128)(2,1)}), bf16[8,256,256]{2,1,0:T(8,128)(2,1)S(1)}, u32[]{:S(2)}, u32[]{:S(2)}) async-start(bf16[8,256,256]{2,1,0:T(8,128)(2,1)} %bitcast.150), calls=%async_computation.1 | async-start | bytes 2097152 | tf_op jit(solution)/shard_map/all_to_all | solution.py:37
  53.6 86.1 %copy-start.3 = (s32[256,2]{0,1:T(2,128)S(1)}, s32[256,2]{0,1:T(2,128)}, u32[]{:S(2)}) copy-start(s32[256,2]{0,1:T(2,128)} %param.23) | copy-start | bytes 6148
  56.9 111.0 %copy-start.1 = (bf16[64,1024]{1,0:T(8,128)(2,1)S(1)}, bf16[64,1024]{1,0:T(8,128)(2,1)}, u32[]{:S(2)}) copy-start(bf16[64,1024]{1,0:T(8,128)(2,1)} %param.15) | copy-start | bytes 393220
  135.0 46.6 %copy-start.2 = (f32[4096]{0:T(1024)S(1)}, f32[4096]{0:T(1024)}, u32[]{:S(2)}) copy-start(f32[4096]{0:T(1024)} %param.21) | copy-start | bytes 49156
  135.0 32.6 %all-to-all-start.2 = ((bf16[16,64,1024]{2,1,0:T(8,128)(2,1)}), bf16[16,64,1024]{2,1,0:T(8,128)(2,1)S(1)}, u32[]{:S(2)}, u32[]{:S(2)}) async-start(bf16[16,64,1024]{2,1,0:T(8,128)(2,1)} %get-tuple-element.130), calls=%async_computation.2 | async-start | bytes 4194304 | tf_op jit(solution)/shard_map/all_to_all | solution.py:37
  168.8 12.3 %all-to-all-start.3 = ((bf16[4,64,1024]{2,1,0:T(8,128)(2,1)}), bf16[4,64,1024]{2,1,0:T(8,128)(2,1)S(1)}, u32[]{:S(2)}, u32[]{:S(2)}) async-start(bf16[4,64,1024]{2,1,0:T(8,128)(2,1)} %stack.2), calls=%async_computation.3 | async-start | bytes 1048576 | tf_op jit(solution)/shard_map/all_to_all | solution.py:187
  183.4 25.1 %all-to-all-start.4 = ((bf16[4,48,4096]{2,1,0:T(8,128)(2,1)}), bf16[4,48,4096]{2,1,0:T(8,128)(2,1)}, u32[]{:S(2)}, u32[]{:S(2)}) async-start(bf16[4,48,4096]{2,1,0:T(8,128)(2,1)} %bitcast.148), calls=%async_computation.4 | async-start | bytes 3145728 | tf_op jit(solution)/shard_map/all_to_all | solution.py:201
  228.5 24.5 %all-to-all-start.5 = ((bf16[4,1,4,48,1024]{4,3,2,1,0:T(8,128)(2,1)}), bf16[4,1,4,48,1024]{4,3,2,1,0:T(8,128)(2,1)}, u32[]{:S(2)}, u32[]{:S(2)}) async-start(bf16[4,1,4,48,1024]{4,3,2,1,0:T(8,128)(2,1)} %copy.63), calls=%async_computation.5 | async-start | bytes 3145728 | tf_op jit(solution)/shard_map/all_to_all | solution.py:37
  255.5 11.5 %all-to-all-start.6 = ((bf16[1,4,48,1024]{3,2,0,1:T(8,128)(2,1)}), bf16[1,4,48,1024]{3,2,0,1:T(8,128)(2,1)S(1)}, u32[]{:S(2)}, u32[]{:S(2)}) async-start(bf16[1,4,48,1024]{3,2,0,1:T(8,128)(2,1)} %bitcast.31), calls=%async_computation.6 | async-start | bytes 786432 | tf_op jit(solution)/shard_map/all_to_all | solution.py:203
